TPU v7x, 32 devices: a whole 2x2x4 slice. The times are simulated.
32 devices in a mesh: gz: 2 (over x), gy: 4 (over y, core), gx: 4 (over z).
Axes of the slice: x: 2, y: 2, z: 4, core: 2. Of those that a mesh axis runs over, the one named last changes fastest.
Arguments:
- density: float32 [32, 64, 256], P('gx', 'gy', 'gz'), may hold values from 0.05 to 0.95
- spread: float32 [32, 64, 256], P('gx', 'gy', 'gz'), may hold values from 0.05 to 0.3
- sensitivities: float32 [9, 32, 64, 256], P(None, 'gx', 'gy', 'gz'), may hold values from -180 to 180, as said below
- violation: float32 [9], replicated, may hold values from -0.05 to 0.15
- multipliers_start: float32 [9], replicated, may hold values from 0.1 to 10
Outputs:
- new_density: float32 [32, 64, 256], P('gx', 'gy', 'gz')
- multipliers: float32 [9], replicated
Inputs may be any that keep to these rules, and one draw needn't show every extreme that they name: `sensitivities`: Real-valued, independent from voxel to voxel.
All inputs are finite; a program needn't handle non-finite values.
Results may differ from a plain program's by a relative error of at most 0.0003.
Values sent between devices are 32-bit elements; how exact they have to be, the bound alone decides.
A program may use at most 64 MiB of HBM per device.

v0:
```python
import math
import jax
import jax.numpy as jnp
from jax import lax
from jax.sharding import PartitionSpec as P

FIELDS = 9
ITERS = 3
RADIUS = 3.0
RAA = 1e-05
MOVE = 0.9
REG = 0.001
FLOOR = 0.2


def padded_2(block, sides, width):
    for axis, dim in sides:
        count = lax.axis_size(axis)
        forward = [(i, i + 1) for i in range(count - 1)]
        backward = [(target, source) for source, target in forward]
        low = lax.ppermute(
            lax.slice_in_dim(block, block.shape[dim] - width, None, axis=dim), axis, forward
        )
        high = lax.ppermute(lax.slice_in_dim(block, 0, width, axis=dim), axis, backward)
        block = jnp.concatenate([low, block, high], axis=dim)
    return block


def smooth(padded, nx, ny, nz):
    total = None
    for a in (-1, 0, 1):
        for b in (-1, 0, 1):
            for c in (-1, 0, 1):
                weight = RADIUS - math.sqrt(a * a + b * b + c * c)
                piece = padded[..., 1 + a : 1 + a + nx, 1 + b : 1 + b + ny, 1 + c : 1 + c + nz]
                total = weight * piece if total is None else total + weight * piece
    return total


def inside(index, extent, count):
    first = (index > 0).astype(jnp.float32)
    last = (index < extent - 1).astype(jnp.float32)
    return jnp.concatenate([first[None], jnp.ones((count,), jnp.float32), last[None]])


def totals(gradient_part, schur_part):
    return lax.psum((gradient_part, schur_part), ("gz", "gy", "gx"))


def shards(density, spread, sensitivities, violation, multipliers_start):
    nx, ny, nz = density.shape
    padded = padded_2(sensitivities, (("gz", 3), ("gy", 2), ("gx", 1)), 1)
    mask_x = inside(lax.axis_index("gx"), lax.axis_size("gx"), nx)
    mask_y = inside(lax.axis_index("gy"), lax.axis_size("gy"), ny)
    mask_z = inside(lax.axis_index("gz"), lax.axis_size("gz"), nz)
    valid = mask_x[:, None, None] * mask_y[None, :, None] * mask_z[None, None, :]
    denom = smooth(valid, nx, ny, nz)
    filtered = smooth(padded, nx, ny, nz) / denom[None]
    cells = nx * ny * nz
    dens = density.reshape(-1)
    span = spread.reshape(-1)
    rows = jnp.concatenate(
        [filtered.reshape(FIELDS, cells), jnp.ones((1, cells), jnp.float32)], axis=0
    )
    grow = jnp.maximum(rows, 0.0)
    fall = jnp.maximum(-rows, 0.0)
    square = span * span
    pp = square * (1.001 * grow + 0.001 * fall + RAA)
    qq = square * (0.001 * grow + 1.001 * fall + RAA)
    lower = dens - span
    upper = dens + span
    floor_x = jnp.maximum(0.0, dens - MOVE * span)
    ceil_x = jnp.minimum(1.0, dens + MOVE * span)
    base = (pp[1:] + qq[1:]) / span
    keep = 1.0 - violation
    base_local = jnp.sum(base, axis=1)
    bound = None
    bound = keep * lax.psum(base_local, ("gz", "gy", "gx"))

    def respond(lam):
        weights = jnp.concatenate([jnp.ones((1,), jnp.float32), lam])
        big_p = jnp.dot(weights, pp, precision=lax.Precision.HIGHEST)
        big_q = jnp.dot(weights, qq, precision=lax.Precision.HIGHEST)
        root_p = jnp.sqrt(big_p)
        root_q = jnp.sqrt(big_q)
        moved = (root_p * lower + root_q * upper) / (root_p + root_q)
        return (jnp.clip(moved, floor_x, ceil_x), big_p, big_q)

    lam = multipliers_start
    for step in range(ITERS):
        moved, big_p, big_q = respond(lam)
        above = upper - moved
        below = moved - lower
        values = pp[1:] / above + qq[1:] / below
        slopes = pp[1:] / (above * above) - qq[1:] / (below * below)
        curv = 2.0 * big_p / (above * above * above) + 2.0 * big_q / (below * below * below)
        schur_part = jnp.dot(slopes / curv, slopes.T, precision=lax.Precision.HIGHEST)
        summed, schur = totals(jnp.sum(values, axis=1), schur_part)
        gradient = summed - bound
        shift = REG * jnp.trace(schur) / FIELDS
        system = schur + shift * jnp.eye(FIELDS, dtype=jnp.float32)
        factor = jnp.linalg.cholesky(system)
        delta = jax.scipy.linalg.cho_solve((factor, True), gradient)
        lam = jnp.maximum(lam + delta, FLOOR * lam)
    moved, big_p, big_q = respond(lam)
    return (moved.reshape(nx, ny, nz), lam)


def solution(mesh):
    return jax.shard_map(
        shards,
        mesh=mesh,
        in_specs=(P("gx", "gy", "gz"), P("gx", "gy", "gz"), P(None, "gx", "gy", "gz"), P(), P()),
        out_specs=(P("gx", "gy", "gz"), P()),
        check_vma=False,
    )
```

profile of v0, /device:TPU:0, one launch (start us, length us, event | category | flops | bytes accessed | tf_op | source)
XLA Modules:
  0.0 187.6 jit_solution(5219307162577140861)
XLA Ops:
  0.6 1.5 fusion.136
  2.7 4.9 %collective-permute-start = (f32[9,8,16,1]{2,1,3,0:T(8,128)S(1)}, f32[9,8,16,1]{2,1,3,0:T(8,128)S(1)}, u32[]{:S(2)}, u32[]{:S(2)}) collective-permute-start(f32[9,8,16,1]{2,1,3,0:T(8,128)S(1)} %copy.82), channel_id=1, source_target_pairs={{0,16},{1,17},{2,18},{3,19},{4,20},{5,21},{6,22},{7,23},{8,24},{9,... | collective-permute-start | bytes 13832 | tf_op jit(solution)/shard_map/ppermute | solution.py:21
  8.0 1.3 collective-permute-start.1
  10.5 3.4 %collective-permute-done.1 = f32[9,8,16,1]{2,1,3,0:T(8,128)S(1)} collective-permute-done((f32[9,8,16,1]{2,1,3,0:T(8,128)S(1)}, f32[9,8,16,1]{2,1,3,0:T(8,128)S(1)}, u32[]{:S(2)}, u32[]{:S(2)}) %collective-permute-start.1) | collective-permute-done | bytes 4640 | tf_op jit(solution)/shard_map/ppermute | solution.py:24
  14.5 1.3 collective-permute-start.2
  15.8 1.3 collective-permute-start.3
  17.5 3.2 %collective-permute-done.3 = f32[9,8,1,130]{3,1,2,0:T(8,128)S(1)} collective-permute-done((f32[9,8,1,130]{3,1,2,0:T(8,128)S(1)}, f32[9,8,1,130]{3,1,2,0:T(8,128)S(1)}, u32[]{:S(2)}, u32[]{:S(2)}) %collective-permute-start.3) | collective-permute-done | bytes 37472 | tf_op jit(solution)/shard_map/ppermute | solution.py:24
  20.7 1.0 pad_maximum_fusion.8
  21.7 3.5 %collective-permute-start.4 = (f32[9,1,18,130]{3,2,1,0:T(8,128)S(1)}, f32[9,1,18,130]{3,2,1,0:T(8,128)S(1)}, u32[]{:S(2)}, u32[]{:S(2)}) collective-permute-start(f32[9,1,18,130]{3,2,1,0:T(8,128)S(1)} %copy.60), channel_id=1, source_target_pairs={{0,1},{1,2},{2,3},{4,5},{5,6},{6,7},{8,9},{9,10},{10,11},{12,13},{... | collective-permute-start | bytes 252728 | tf_op jit(solution)/shard_map/ppermute | solution.py:21
  25.3 1.5 collective-permute-start.5
  26.7 1.0 maximum_maximum_fusion.1
  27.7 1.3 collective-permute-done.4
  29.2 4.5 %collective-permute-done.5 = f32[9,1,18,130]{3,2,1,0:T(8,128)S(1)} collective-permute-done((f32[9,1,18,130]{3,2,1,0:T(8,128)S(1)}, f32[9,1,18,130]{3,2,1,0:T(8,128)S(1)}, u32[]{:S(2)}, u32[]{:S(2)}) %collective-permute-start.5) | collective-permute-done | bytes 84272 | tf_op jit(solution)/shard_map/ppermute | solution.py:24
  33.9 2.1 %maximum_maximum_fusion = (f32[9,9,18,130]{3,1,2,0:T(8,128)S(1)}, f32[9,9,18,130]{3,1,2,0:T(8,128)S(1)}) fusion(f32[9,8,1,130]{3,1,2,0:T(8,128)S(1)} %collective-permute-done.3, f32[9,8,16,1]{3,1,2,0:T(8,128)S(1)} %copy.59, f32[9,8,16,128]{3,1,2,0:T(8,128)S(1)} %copy.58, f32[9,8,16,1]{3,1,2,0:T(8,128)S(1)} %copy.57, ...), kind=kLoop, calls=%fused_computation | loop fusion | flops 1895400 | bytes 2358720 | tf_op jit(solution)/shard_map/concatenate | solution.py:25
  36.0 3.1 %fusion.29 = f32[9,8,16,128]{3,1,2,0:T(8,128)S(1)} fusion(f32[9,9,18,130]{3,1,2,0:T(8,128)S(1)} %get-tuple-element.33, f32[9,8,17,130]{3,1,2,0:T(8,128)S(1)} %get-tuple-element.37, f32[9,8,16,1]{3,1,2,0:T(8,128)S(1)} %copy.59, f32[9,8,16,128]{3,1,2,0:T(8,128)S(1)} %copy.58, f32[9,8,16,1]{3,1,2,0:T(8,128)S(1)} %copy.57, ...), kind=kLoop, calls=%fused_computation.47 | loop fusion | flops 8257536 | bytes 15410176 | tf_op jit(solution)/shard_map/div | solution.py:58
  39.4 0.6 copy.84
  40.0 0.5 add_multiply_fusion.1
  40.5 0.6 fusion.122
  41.2 0.6 fusion.124
  41.9 0.8 fusion.21
  42.8 1.7 fusion.4
  44.5 40.1 %all-reduce.3 = (f32[9,9]{0,1:T(8,128)S(1)}, f32[9]{0:T(128)S(1)}, f32[9]{0:T(128)S(1)}) all-reduce(f32[9,9]{0,1:T(8,128)S(1)} %fusion.4, f32[9]{0:T(128)S(1)} %get-tuple-element.5, f32[9]{0:T(128)S(1)} %get-tuple-element.4), channel_id=1, replica_groups=mesh['gz'=2,'gy'=4,'gx'=4] {'gz','gy','gx'}, use_global_device_ids=true, to_apply=%region_0.0 | all-reduce | flops 99 | bytes 792 | tf_op jit(solution)/shard_map/psum | solution.py:47
  84.6 0.6 select_reduce_fusion.5
  86.0 0.8 cholesky.59
  86.8 0.6 compare_reduce_fusion.2
  87.5 0.6 fusion.92
  88.1 0.7 custom-call.9
  89.1 0.7 fusion.120
  89.8 0.6 fusion.118
  91.0 1.7 fusion.2
  92.7 40.2 %all-reduce.2 = (f32[9,9]{0,1:T(8,128)S(1)}, f32[9]{0:T(128)S(1)}) all-reduce(f32[9,9]{0,1:T(8,128)S(1)} %fusion.2, f32[9]{0:T(128)S(1)} %add_reduce_fusion.1), channel_id=1, replica_groups=mesh['gz'=2,'gy'=4,'gx'=4] {'gz','gy','gx'}, use_global_device_ids=true, to_apply=%region_8.11 | all-reduce | flops 90 | bytes 720 | tf_op jit(solution)/shard_map/psum | solution.py:47
  132.9 0.6 select_reduce_fusion.4
  134.2 0.8 cholesky.70
  135.1 0.6 compare_reduce_fusion.1
  135.7 0.6 fusion.93
  136.4 0.7 custom-call.10
  137.4 0.7 fusion.116
  138.0 0.6 fusion.114
  139.3 1.7 fusion
  140.9 40.1 %all-reduce.1 = (f32[9,9]{0,1:T(8,128)S(1)}, f32[9]{0:T(128)S(1)}) all-reduce(f32[9,9]{0,1:T(8,128)S(1)} %fusion, f32[9]{0:T(128)S(1)} %add_reduce_fusion), channel_id=1, replica_groups=mesh['gz'=2,'gy'=4,'gx'=4] {'gz','gy','gx'}, use_global_device_ids=true, to_apply=%region_12.15 | all-reduce | flops 90 | bytes 720 | tf_op jit(solution)/shard_map/psum | solution.py:47
  181.1 0.6 select_reduce_fusion.3
  182.4 0.8 cholesky.81
  183.3 0.6 compare_reduce_fusion
  183.9 0.6 fusion.94
  184.6 0.7 custom-call.11
  185.6 0.7 fusion.128
  186.2 0.6 fusion.126
  186.9 0.7 maximum_minimum_fusion
  (65 shorter events, 6.3 us)
Async XLA Ops:
  0.6 9.2 %copy-start = (f32[9,8,16,128]{3,2,1,0:T(8,128)S(1)}, f32[9,8,16,128]{3,2,1,0:T(8,128)}, u32[]{:S(2)}) copy-start(f32[9,8,16,128]{3,2,1,0:T(8,128)} %param.10) | copy-start | bytes 1769476
  2.7 7.4 %collective-permute-start = (f32[9,8,16,1]{2,1,3,0:T(8,128)S(1)}, f32[9,8,16,1]{2,1,3,0:T(8,128)S(1)}, u32[]{:S(2)}, u32[]{:S(2)}) collective-permute-start(f32[9,8,16,1]{2,1,3,0:T(8,128)S(1)} %copy.82), channel_id=1, source_target_pairs={{0,16},{1,17},{2,18},{3,19},{4,20},{5,21},{6,22},{7,23},{8,24},{9,... | collective-permute-start | bytes 13832 | tf_op jit(solution)/shard_map/ppermute | solution.py:21
  8.0 5.9 %collective-permute-start.1 = (f32[9,8,16,1]{2,1,3,0:T(8,128)S(1)}, f32[9,8,16,1]{2,1,3,0:T(8,128)S(1)}, u32[]{:S(2)}, u32[]{:S(2)}) collective-permute-start(f32[9,8,16,1]{2,1,3,0:T(8,128)S(1)} %copy.83), channel_id=1, source_target_pairs={{16,0},{17,1},{18,2},{19,3},{20,4},{21,5},{22,6},{23,7},{24,8},{25... | collective-permute-start | bytes 13832 | tf_op jit(solution)/shard_map/ppermute | solution.py:24
  10.0 7.5 %copy-start.1 = (f32[8,16,128]{2,1,0:T(8,128)S(1)}, f32[8,16,128]{2,1,0:T(8,128)}, u32[]{:S(2)}) copy-start(f32[8,16,128]{2,1,0:T(8,128)} %param.9) | copy-start | bytes 196612
  14.5 3.0 %collective-permute-start.2 = (f32[9,8,1,130]{3,1,2,0:T(8,128)S(1)}, f32[9,8,1,130]{3,1,2,0:T(8,128)S(1)}, u32[]{:S(2)}, u32[]{:S(2)}) collective-permute-start(f32[9,8,1,130]{3,1,2,0:T(8,128)S(1)} %get-tuple-element.38), channel_id=1, source_target_pairs={{0,4},{4,8},{8,12},{1,5},{5,9},{9,13},{2,6},{6,10},{10,14},{3,7},{... | collective-permute-start | bytes 112328 | tf_op jit(solution)/shard_map/ppermute | solution.py:21
  15.8 4.9 %collective-permute-start.3 = (f32[9,8,1,130]{3,1,2,0:T(8,128)S(1)}, f32[9,8,1,130]{3,1,2,0:T(8,128)S(1)}, u32[]{:S(2)}, u32[]{:S(2)}) collective-permute-start(f32[9,8,1,130]{3,1,2,0:T(8,128)S(1)} %get-tuple-element.39), channel_id=1, source_target_pairs={{4,0},{8,4},{12,8},{5,1},{9,5},{13,9},{6,2},{10,6},{14,10},{7,3},{... | collective-permute-start | bytes 112328 | tf_op jit(solution)/shard_map/ppermute | solution.py:24
  21.7 7.3 %collective-permute-start.4 = (f32[9,1,18,130]{3,2,1,0:T(8,128)S(1)}, f32[9,1,18,130]{3,2,1,0:T(8,128)S(1)}, u32[]{:S(2)}, u32[]{:S(2)}) collective-permute-start(f32[9,1,18,130]{3,2,1,0:T(8,128)S(1)} %copy.60), channel_id=1, source_target_pairs={{0,1},{1,2},{2,3},{4,5},{5,6},{6,7},{8,9},{9,10},{10,11},{12,13},{... | collective-permute-start | bytes 252728 | tf_op jit(solution)/shard_map/ppermute | solution.py:21
  25.3 8.4 %collective-permute-start.5 = (f32[9,1,18,130]{3,2,1,0:T(8,128)S(1)}, f32[9,1,18,130]{3,2,1,0:T(8,128)S(1)}, u32[]{:S(2)}, u32[]{:S(2)}) collective-permute-start(f32[9,1,18,130]{3,2,1,0:T(8,128)S(1)} %copy.67), channel_id=1, source_target_pairs={{1,0},{2,1},{3,2},{5,4},{6,5},{7,6},{9,8},{10,9},{11,10},{13,12},{... | collective-permute-start | bytes 252728 | tf_op jit(solution)/shard_map/ppermute | solution.py:24
  39.3 1.2 copy-start.3
  40.0 1.8 copy-start.2
  42.8 46.0 %copy-start.5 = (f32[9]{0:T(128)S(1)}, f32[9]{0:T(128)}, u32[]{:S(2)}) copy-start(f32[9]{0:T(128)} %param.11) | copy-start | bytes 112
  185.6 2.0 %copy-start.4 = (f32[9]{0:T(128)}, f32[9]{0:T(128)S(1)}, u32[]{:S(2)}) copy-start(f32[9]{0:T(128)S(1)} %fusion.11) | copy-start | bytes 112
where the time goes:
time: 188 us
  blocking collectives  120 us (64%)
  other arithmetic  21.8 us (12%)
  starting transfers between devices  13.7 us (7%)
  waiting for transfers between devices  12.4 us (7%)
  matrix products  11 us (6%)
  local copies, waits for them, and re-layouts  5.18 us (3%)
  between operations  3.06 us (2%)
    psum x3, blocking collectives, totals(): return lax.psum((gradient_part, schur_part), ('gz', 'gy', 'gx'))  120 us
    ppermute x3, waiting for transfers between devices, padded_2(): lax.ppermute(lax.slice_in_dim(block, 0, width, axis=dim), axis, backward)  11.1 us
    ppermute x3, starting transfers between devices, padded_2(): lax.ppermute(lax.slice_in_dim(block, block.shape[dim] - width, None, axis...  9.67 us
    dot_general x3, matrix products, shards(): jnp.dot(slopes / curv, slopes.T, precision=lax.Precision.HIGHEST)  5.02 us
    another operation x9, other arithmetic, shards(): factor = jnp.linalg.cholesky(system)  4.45 us
    ppermute x3, starting transfers between devices, padded_2(): lax.ppermute(lax.slice_in_dim(block, 0, width, axis=dim), axis, backward)  4.06 us
    another operation x6, other arithmetic, shards(): delta = jax.scipy.linalg.cho_solve((factor, True), gradient)  4.03 us
  transfers between devices with their start and end apart: 6, of which 4 were waited for; matrix products, arithmetic and copies ran while one was open for 2% of the time, Pallas kernels for 0%

commit v1 on v0

--- a/solution.py
+++ b/solution.py
@@ -11,6 +11,11 @@
 MOVE = 0.9
 REG = 0.001
 FLOOR = 0.2
+
+
+def one_after_other(array, one, other):
+    partial = lax.psum(array, one)
+    return lax.psum(partial, other)
 
 
 def padded_2(block, sides, width):
@@ -44,7 +49,7 @@
 
 
 def totals(gradient_part, schur_part):
-    return lax.psum((gradient_part, schur_part), ("gz", "gy", "gx"))
+    return one_after_other((gradient_part, schur_part), "gz", ("gy", "gx"))
 
 
 def shards(density, spread, sensitivities, violation, multipliers_start):

time: 188 us -> 219 us (1.16)
  blocking collectives: 120 us -> 151 us
    psum x3 -> x7, blocking collectives: 120 us -> 151 us  [the longest x3 96.8 us: one_after_other(): return lax.psum(partial, other)]
  transfers between devices with their start and end apart: 6 -> 6, of which waited for: 4 -> 4; matrix products, arithmetic and copies ran while one was open for 2% -> 1% of each run, Pallas kernels for 0% -> 0%
where the time goes in v1:
time: 219 us
  blocking collectives  151 us (69%)
  other arithmetic  21.8 us (10%)
  starting transfers between devices  13.7 us (6%)
  waiting for transfers between devices  12.4 us (6%)
  matrix products  11 us (5%)
  local copies, waits for them, and re-layouts  5.18 us (2%)
  between operations  3.08 us (1%)
    psum x3, blocking collectives, one_after_other(): return lax.psum(partial, other)  96.8 us
    psum x1, blocking collectives, shards(): bound = keep * lax.psum(base_local, ('gz', 'gy', 'gx'))  39 us
    psum x3, blocking collectives, one_after_other(): partial = lax.psum(array, one)  15.5 us
    ppermute x3, waiting for transfers between devices, padded_2(): lax.ppermute(lax.slice_in_dim(block, 0, width, axis=dim), axis, backward)  11.1 us
    ppermute x3, starting transfers between devices, padded_2(): lax.ppermute(lax.slice_in_dim(block, block.shape[dim] - width, None, axis...  9.67 us
    dot_general x3, matrix products, shards(): jnp.dot(slopes / curv, slopes.T, precision=lax.Precision.HIGHEST)  5.02 us
    another operation x9, other arithmetic, shards(): factor = jnp.linalg.cholesky(system)  4.45 us
  transfers between devices with their start and end apart: 6, of which 4 were waited for; matrix products, arithmetic and copies ran while one was open for 1% of the time, Pallas kernels for 0%

profile of v1, /device:TPU:0, one launch (start us, length us, event | category | flops | bytes accessed | tf_op | source)
XLA Modules:
  0.0 218.5 jit_solution(14672688335127884761)
XLA Ops:
  0.6 1.5 fusion.136
  2.7 4.9 %collective-permute-start = (f32[9,8,16,1]{2,1,3,0:T(8,128)S(1)}, f32[9,8,16,1]{2,1,3,0:T(8,128)S(1)}, u32[]{:S(2)}, u32[]{:S(2)}) collective-permute-start(f32[9,8,16,1]{2,1,3,0:T(8,128)S(1)} %copy.82), channel_id=1, source_target_pairs={{0,16},{1,17},{2,18},{3,19},{4,20},{5,21},{6,22},{7,23},{8,24},{9,... | collective-permute-start | bytes 13832 | tf_op jit(solution)/shard_map/ppermute | solution.py:26
  8.0 1.3 collective-permute-start.1
  10.5 3.4 %collective-permute-done.1 = f32[9,8,16,1]{2,1,3,0:T(8,128)S(1)} collective-permute-done((f32[9,8,16,1]{2,1,3,0:T(8,128)S(1)}, f32[9,8,16,1]{2,1,3,0:T(8,128)S(1)}, u32[]{:S(2)}, u32[]{:S(2)}) %collective-permute-start.1) | collective-permute-done | bytes 4640 | tf_op jit(solution)/shard_map/ppermute | solution.py:29
  14.5 1.3 collective-permute-start.2
  15.8 1.3 collective-permute-start.3
  17.5 3.2 %collective-permute-done.3 = f32[9,8,1,130]{3,1,2,0:T(8,128)S(1)} collective-permute-done((f32[9,8,1,130]{3,1,2,0:T(8,128)S(1)}, f32[9,8,1,130]{3,1,2,0:T(8,128)S(1)}, u32[]{:S(2)}, u32[]{:S(2)}) %collective-permute-start.3) | collective-permute-done | bytes 37472 | tf_op jit(solution)/shard_map/ppermute | solution.py:29
  20.7 1.0 pad_maximum_fusion.8
  21.7 3.5 %collective-permute-start.4 = (f32[9,1,18,130]{3,2,1,0:T(8,128)S(1)}, f32[9,1,18,130]{3,2,1,0:T(8,128)S(1)}, u32[]{:S(2)}, u32[]{:S(2)}) collective-permute-start(f32[9,1,18,130]{3,2,1,0:T(8,128)S(1)} %copy.60), channel_id=1, source_target_pairs={{0,1},{1,2},{2,3},{4,5},{5,6},{6,7},{8,9},{9,10},{10,11},{12,13},{... | collective-permute-start | bytes 252728 | tf_op jit(solution)/shard_map/ppermute | solution.py:26
  25.3 1.5 collective-permute-start.5
  26.7 1.0 maximum_maximum_fusion.1
  27.7 1.3 collective-permute-done.4
  29.2 4.5 %collective-permute-done.5 = f32[9,1,18,130]{3,2,1,0:T(8,128)S(1)} collective-permute-done((f32[9,1,18,130]{3,2,1,0:T(8,128)S(1)}, f32[9,1,18,130]{3,2,1,0:T(8,128)S(1)}, u32[]{:S(2)}, u32[]{:S(2)}) %collective-permute-start.5) | collective-permute-done | bytes 84272 | tf_op jit(solution)/shard_map/ppermute | solution.py:29
  33.9 2.1 maximum_maximum_fusion
  36.0 3.1 %fusion.29 = f32[9,8,16,128]{3,1,2,0:T(8,128)S(1)} fusion(f32[9,9,18,130]{3,1,2,0:T(8,128)S(1)} %get-tuple-element.38, f32[9,8,17,130]{3,1,2,0:T(8,128)S(1)} %get-tuple-element.42, f32[9,8,16,1]{3,1,2,0:T(8,128)S(1)} %copy.59, f32[9,8,16,128]{3,1,2,0:T(8,128)S(1)} %copy.58, f32[9,8,16,1]{3,1,2,0:T(8,128)S(1)} %copy.57, ...), kind=kLoop, calls=%fused_computation.47 | loop fusion | flops 8257536 | bytes 15410176 | tf_op jit(solution)/shard_map/div | solution.py:63
  39.4 0.6 copy.84
  40.5 0.6 fusion.122
  41.2 0.6 fusion.124
  41.9 0.8 fusion.21
  42.8 1.7 fusion.4
  44.5 5.0 %all-reduce.6 = (f32[9,9]{0,1:T(8,128)S(1)}, f32[9]{0:T(128)S(1)}) all-reduce(f32[9,9]{0,1:T(8,128)S(1)} %fusion.4, f32[9]{0:T(128)S(1)} %get-tuple-element.5), channel_id=1, replica_groups=mesh['gz'=2,'gy'=4,'gx'=4] {'gz'}, use_global_device_ids=true, to_apply=%region_0.0 | all-reduce | flops 90 | bytes 720 | tf_op jit(solution)/shard_map/psum | solution.py:17
  49.5 32.6 %all-reduce.3 = (f32[9,9]{0,1:T(8,128)S(1)}, f32[9]{0:T(128)S(1)}) all-reduce(f32[9,9]{0,1:T(8,128)S(1)} %get-tuple-element.16, f32[9]{0:T(128)S(1)} %get-tuple-element.17), channel_id=1, replica_groups=mesh['gz'=2,'gy'=4,'gx'=4] {'gy','gx'}, use_global_device_ids=true, to_apply=%region_1.0 | all-reduce | flops 90 | bytes 720 | tf_op jit(solution)/shard_map/psum | solution.py:18
  83.5 0.8 cholesky.59
  84.3 0.6 compare_reduce_fusion.2
  85.0 0.6 fusion.92
  85.6 0.7 custom-call.9
  86.3 39.0 %psum.95 = f32[9]{0:T(128)S(1)} all-reduce(f32[9]{0:T(128)S(1)} %get-tuple-element.4), channel_id=1, replica_groups=mesh['gz'=2,'gy'=4,'gx'=4] {'gz','gy','gx'}, use_global_device_ids=true, to_apply=%region_9.11 | all-reduce | flops 9 | bytes 72 | tf_op jit(solution)/shard_map/psum | solution.py:83
  125.6 0.7 fusion.120
  126.3 0.6 fusion.118
  127.5 1.7 fusion.2
  129.2 5.3 %all-reduce.5 = (f32[9,9]{0,1:T(8,128)S(1)}, f32[9]{0:T(128)S(1)}) all-reduce(f32[9,9]{0,1:T(8,128)S(1)} %fusion.2, f32[9]{0:T(128)S(1)} %add_reduce_fusion.1), channel_id=1, replica_groups=mesh['gz'=2,'gy'=4,'gx'=4] {'gz'}, use_global_device_ids=true, to_apply=%region_10.13 | all-reduce | flops 90 | bytes 720 | tf_op jit(solution)/shard_map/psum | solution.py:17
  134.5 32.3 %all-reduce.2 = (f32[9,9]{0,1:T(8,128)S(1)}, f32[9]{0:T(128)S(1)}) all-reduce(f32[9,9]{0,1:T(8,128)S(1)} %get-tuple-element.14, f32[9]{0:T(128)S(1)} %get-tuple-element.15), channel_id=1, replica_groups=mesh['gz'=2,'gy'=4,'gx'=4] {'gy','gx'}, use_global_device_ids=true, to_apply=%region_11.14 | all-reduce | flops 90 | bytes 720 | tf_op jit(solution)/shard_map/psum | solution.py:18
  168.2 0.8 cholesky.70
  169.0 0.6 compare_reduce_fusion.1
  169.7 0.6 fusion.93
  170.3 0.7 custom-call.10
  171.3 0.7 fusion.116
  172.0 0.6 fusion.114
  173.2 1.7 fusion
  174.9 5.2 %all-reduce.4 = (f32[9,9]{0,1:T(8,128)S(1)}, f32[9]{0:T(128)S(1)}) all-reduce(f32[9,9]{0,1:T(8,128)S(1)} %fusion, f32[9]{0:T(128)S(1)} %add_reduce_fusion), channel_id=1, replica_groups=mesh['gz'=2,'gy'=4,'gx'=4] {'gz'}, use_global_device_ids=true, to_apply=%region_16.19 | all-reduce | flops 90 | bytes 720 | tf_op jit(solution)/shard_map/psum | solution.py:17
  180.1 31.9 %all-reduce.1 = (f32[9,9]{0,1:T(8,128)S(1)}, f32[9]{0:T(128)S(1)}) all-reduce(f32[9,9]{0,1:T(8,128)S(1)} %get-tuple-element.12, f32[9]{0:T(128)S(1)} %get-tuple-element.13), channel_id=1, replica_groups=mesh['gz'=2,'gy'=4,'gx'=4] {'gy','gx'}, use_global_device_ids=true, to_apply=%region_17.20 | all-reduce | flops 90 | bytes 720 | tf_op jit(solution)/shard_map/psum | solution.py:18
  213.4 0.8 cholesky.81
  214.2 0.6 compare_reduce_fusion
  214.9 0.6 fusion.94
  215.5 0.7 custom-call.11
  216.5 0.7 fusion.128
  217.2 0.6 fusion.126
  217.8 0.7 maximum_minimum_fusion
  (69 shorter events, 8.6 us)
Async XLA Ops:
  0.6 9.2 %copy-start = (f32[9,8,16,128]{3,2,1,0:T(8,128)S(1)}, f32[9,8,16,128]{3,2,1,0:T(8,128)}, u32[]{:S(2)}) copy-start(f32[9,8,16,128]{3,2,1,0:T(8,128)} %param.10) | copy-start | bytes 1769476
  2.7 7.4 %collective-permute-start = (f32[9,8,16,1]{2,1,3,0:T(8,128)S(1)}, f32[9,8,16,1]{2,1,3,0:T(8,128)S(1)}, u32[]{:S(2)}, u32[]{:S(2)}) collective-permute-start(f32[9,8,16,1]{2,1,3,0:T(8,128)S(1)} %copy.82), channel_id=1, source_target_pairs={{0,16},{1,17},{2,18},{3,19},{4,20},{5,21},{6,22},{7,23},{8,24},{9,... | collective-permute-start | bytes 13832 | tf_op jit(solution)/shard_map/ppermute | solution.py:26
  8.0 5.9 %collective-permute-start.1 = (f32[9,8,16,1]{2,1,3,0:T(8,128)S(1)}, f32[9,8,16,1]{2,1,3,0:T(8,128)S(1)}, u32[]{:S(2)}, u32[]{:S(2)}) collective-permute-start(f32[9,8,16,1]{2,1,3,0:T(8,128)S(1)} %copy.83), channel_id=1, source_target_pairs={{16,0},{17,1},{18,2},{19,3},{20,4},{21,5},{22,6},{23,7},{24,8},{25... | collective-permute-start | bytes 13832 | tf_op jit(solution)/shard_map/ppermute | solution.py:29
  10.0 7.5 %copy-start.1 = (f32[8,16,128]{2,1,0:T(8,128)S(1)}, f32[8,16,128]{2,1,0:T(8,128)}, u32[]{:S(2)}) copy-start(f32[8,16,128]{2,1,0:T(8,128)} %param.9) | copy-start | bytes 196612
  14.5 3.0 %collective-permute-start.2 = (f32[9,8,1,130]{3,1,2,0:T(8,128)S(1)}, f32[9,8,1,130]{3,1,2,0:T(8,128)S(1)}, u32[]{:S(2)}, u32[]{:S(2)}) collective-permute-start(f32[9,8,1,130]{3,1,2,0:T(8,128)S(1)} %get-tuple-element.43), channel_id=1, source_target_pairs={{0,4},{4,8},{8,12},{1,5},{5,9},{9,13},{2,6},{6,10},{10,14},{3,7},{... | collective-permute-start | bytes 112328 | tf_op jit(solution)/shard_map/ppermute | solution.py:26
  15.8 4.9 %collective-permute-start.3 = (f32[9,8,1,130]{3,1,2,0:T(8,128)S(1)}, f32[9,8,1,130]{3,1,2,0:T(8,128)S(1)}, u32[]{:S(2)}, u32[]{:S(2)}) collective-permute-start(f32[9,8,1,130]{3,1,2,0:T(8,128)S(1)} %get-tuple-element.44), channel_id=1, source_target_pairs={{4,0},{8,4},{12,8},{5,1},{9,5},{13,9},{6,2},{10,6},{14,10},{7,3},{... | collective-permute-start | bytes 112328 | tf_op jit(solution)/shard_map/ppermute | solution.py:29
  21.7 7.3 %collective-permute-start.4 = (f32[9,1,18,130]{3,2,1,0:T(8,128)S(1)}, f32[9,1,18,130]{3,2,1,0:T(8,128)S(1)}, u32[]{:S(2)}, u32[]{:S(2)}) collective-permute-start(f32[9,1,18,130]{3,2,1,0:T(8,128)S(1)} %copy.60), channel_id=1, source_target_pairs={{0,1},{1,2},{2,3},{4,5},{5,6},{6,7},{8,9},{9,10},{10,11},{12,13},{... | collective-permute-start | bytes 252728 | tf_op jit(solution)/shard_map/ppermute | solution.py:26
  25.3 8.4 %collective-permute-start.5 = (f32[9,1,18,130]{3,2,1,0:T(8,128)S(1)}, f32[9,1,18,130]{3,2,1,0:T(8,128)S(1)}, u32[]{:S(2)}, u32[]{:S(2)}) collective-permute-start(f32[9,1,18,130]{3,2,1,0:T(8,128)S(1)} %copy.67), channel_id=1, source_target_pairs={{1,0},{2,1},{3,2},{5,4},{6,5},{7,6},{9,8},{10,9},{11,10},{13,12},{... | collective-permute-start | bytes 252728 | tf_op jit(solution)/shard_map/ppermute | solution.py:29
  39.3 1.2 copy-start.3
  40.0 1.8 copy-start.2
  42.8 82.5 %copy-start.5 = (f32[9]{0:T(128)S(1)}, f32[9]{0:T(128)}, u32[]{:S(2)}) copy-start(f32[9]{0:T(128)} %param.11) | copy-start | bytes 112
  216.5 2.0 copy-start.4
